TPU v7x, 32 devices: a whole 2x2x4 slice. The times are simulated.
32 devices in a mesh: rep: 4 (over y, x), cp: 8 (over z, core).
Axes of the slice: x: 2, y: 2, z: 4, core: 2. Of those that a mesh axis runs over, the one named last changes fastest.
Arguments:
- tokens: bfloat16 [4, 2048, 768], P('rep', 'cp'), may hold values from -6 to 6
- query_weight: bfloat16 [768, 768], P('cp'), may hold values from -0.3125 to 0.3125
- query_bias: bfloat16 [768], P('cp'), may hold values from -3 to 3
- key_weight: bfloat16 [768, 768], P('cp'), may hold values from -0.3125 to 0.3125
- value_weight: bfloat16 [768, 768], P('cp'), may hold values from -0.21875 to 0.21875
- value_bias: bfloat16 [768], P('cp'), may hold values from -3 to 3
- output_weight: bfloat16 [768, 768], P('cp'), may hold values from -1.5 to 1.5
- output_bias: bfloat16 [768], P('cp'), may hold values from -1.796875 to 1.796875
- first_gain: bfloat16 [768], P('cp'), may hold values from 0.099609375 to 1.8984375
- first_shift: bfloat16 [768], P('cp'), may hold values from -1.796875 to 1.796875
- up_weight: bfloat16 [768, 3072], P('cp'), may hold values from -0.21875 to 0.21875
- up_bias: bfloat16 [3072], P('cp'), may hold values from -3 to 3
- down_weight: bfloat16 [3072, 768], P('cp'), may hold values from -0.109375 to 0.109375
- down_bias: bfloat16 [768], P('cp'), may hold values from -1.796875 to 1.796875
- second_gain: bfloat16 [768], P('cp'), may hold values from 0.099609375 to 1.8984375
- second_shift: bfloat16 [768], P('cp'), may hold values from -1.796875 to 1.796875
- cotangent: float32 [4, 2048, 768], P('rep', 'cp'), may hold values from -18 to 18
Outputs:
- layer_out: float32 [4, 2048, 768], P('rep', 'cp')
- grad_tokens: float32 [4, 2048, 768], P('rep', 'cp')
- grad_query_weight: float32 [768, 768], P('cp')
- grad_query_bias: float32 [768], P('cp')
- grad_key_weight: float32 [768, 768], P('cp')
- grad_value_weight: float32 [768, 768], P('cp')
- grad_value_bias: float32 [768], P('cp')
- grad_output_weight: float32 [768, 768], P('cp')
- grad_output_bias: float32 [768], P('cp')
- grad_first_gain: float32 [768], P('cp')
- grad_first_shift: float32 [768], P('cp')
- grad_up_weight: float32 [768, 3072], P('cp')
- grad_up_bias: float32 [3072], P('cp')
- grad_down_weight: float32 [3072, 768], P('cp')
- grad_down_bias: float32 [768], P('cp')
- grad_second_gain: float32 [768], P('cp')
- grad_second_shift: float32 [768], P('cp')
- rms_values: float32 [1], replicated
All inputs are finite; a program needn't handle non-finite values.
Results may differ from a plain program's by a relative error of at most 0.025.
Values may be sent and summed in bfloat16 or wider, within the bound.
A program may use at most 192 MiB of HBM per device.

v0:
```python
import math
import jax
import jax.numpy as jnp
from jax import lax
from jax.sharding import PartitionSpec as P

H = 12
HD = 64
KEYB = 512
EPSILON = 1e-12


def for_sending(x):
    return jax.tree.map(lambda a: a.astype(jnp.bfloat16) if a.dtype == jnp.float32 else a, x)


def normalize(values, norm_gain, norm_shift):
    center = values - jnp.mean(values, axis=-1, keepdims=True)
    spread = jnp.mean(center * center, axis=-1, keepdims=True)
    return center * lax.rsqrt(spread + EPSILON) * norm_gain + norm_shift


def gelu_exact(values):
    return 0.5 * values * (1.0 + lax.erf(values * (1.0 / math.sqrt(2.0))))


def matmul(left, right):
    return jnp.dot(left, right, preferred_element_type=jnp.float32)


def over_rows(left, right):
    return jnp.einsum("ta,tb->ab", left, right, preferred_element_type=jnp.float32)


def against(left, right):
    return jnp.einsum("ta,ba->tb", left, right, preferred_element_type=jnp.float32)


def column_sum(values):
    return jnp.sum(values.astype(jnp.float32), axis=0)


def head_scores(query_heads, key_heads):
    raw_scores = jnp.einsum(
        "qhd,khd->hqk", query_heads, key_heads, preferred_element_type=jnp.float32
    )
    return raw_scores * (1.0 / math.sqrt(HD))


def probabilities(scores, row_top, row_total):
    return jnp.exp(scores - row_top[:, :, None]) / row_total[:, :, None]


def score_grads(query_heads, grad_heads, key_heads, value_heads, row_top, row_total, row_delta):
    probs = probabilities(head_scores(query_heads, key_heads), row_top, row_total)
    grad_probs = jnp.einsum(
        "qhd,khd->hqk", grad_heads, value_heads, preferred_element_type=jnp.float32
    )
    grad_scores = (probs * (grad_probs - row_delta[:, :, None]) * (1.0 / math.sqrt(HD))).astype(
        jnp.bfloat16
    )
    return (probs.astype(jnp.bfloat16), grad_scores)


def on_device(
    tokens,
    query_weight,
    query_bias,
    key_weight,
    value_weight,
    value_bias,
    output_weight,
    output_bias,
    first_gain,
    first_shift,
    up_weight,
    up_bias,
    down_weight,
    down_bias,
    second_gain,
    second_shift,
    cotangent,
):
    shards = (
        query_weight,
        query_bias,
        key_weight,
        value_weight,
        value_bias,
        output_weight,
        output_bias,
        first_gain,
        first_shift,
        up_weight,
        up_bias,
        down_weight,
        down_bias,
        second_gain,
        second_shift,
    )
    gathered = (
        lax.all_gather(shards[0], "cp", axis=0, tiled=True),
        lax.all_gather(shards[1], "cp", axis=0, tiled=True),
        lax.all_gather(shards[2], "cp", axis=0, tiled=True),
        lax.all_gather(shards[3], "cp", axis=0, tiled=True),
        lax.all_gather(shards[4], "cp", axis=0, tiled=True),
        lax.all_gather(shards[5], "cp", axis=0, tiled=True),
        lax.all_gather(shards[6], "cp", axis=0, tiled=True),
        lax.all_gather(shards[7], "cp", axis=0, tiled=True),
        lax.all_gather(shards[8], "cp", axis=0, tiled=True),
        lax.all_gather(shards[9], "cp", axis=0, tiled=True),
        lax.all_gather(shards[10], "cp", axis=0, tiled=True),
        lax.all_gather(shards[11], "cp", axis=0, tiled=True),
        lax.all_gather(shards[12], "cp", axis=0, tiled=True),
        lax.all_gather(shards[13], "cp", axis=0, tiled=True),
        lax.all_gather(shards[14], "cp", axis=0, tiled=True),
    )
    (
        w_query,
        b_query,
        w_key,
        w_value,
        b_value,
        w_output,
        b_output,
        gain_first,
        shift_first,
        w_up,
        b_up,
        w_down,
        b_down,
        gain_second,
        shift_second,
    ) = gathered
    row_count = tokens.shape[1]
    model_width = tokens.shape[2]
    local_tokens = tokens[0]
    query_rows = (matmul(local_tokens, w_query) + b_query.astype(jnp.float32)).astype(jnp.bfloat16)
    key_rows = matmul(local_tokens, w_key).astype(jnp.bfloat16)
    value_rows = (matmul(local_tokens, w_value) + b_value.astype(jnp.float32)).astype(jnp.bfloat16)
    all_keys, all_values = (
        lax.all_gather(key_rows, "cp", axis=0, tiled=True),
        lax.all_gather(value_rows, "cp", axis=0, tiled=True),
    )
    seq_len = all_keys.shape[0]
    block_len = math.gcd(seq_len, KEYB)
    key_blocks = all_keys.reshape(seq_len // block_len, block_len, H, HD)
    value_blocks = all_values.reshape(seq_len // block_len, block_len, H, HD)
    query_heads = query_rows.reshape(row_count, H, HD)

    def stat_step(carry, key_block):
        old_top, old_total = carry
        scores = head_scores(query_heads, key_block)
        new_top = jnp.maximum(old_top, jnp.max(scores, axis=-1))
        new_total = old_total * jnp.exp(old_top - new_top) + jnp.sum(
            jnp.exp(scores - new_top[:, :, None]), axis=-1
        )
        return ((new_top, new_total), None)

    start_top = jnp.full((H, row_count), -jnp.inf, jnp.float32)
    start_total = jnp.zeros((H, row_count), jnp.float32)
    (row_top, row_total), _ = lax.scan(stat_step, (start_top, start_total), key_blocks)

    def value_step(carry, blocks):
        key_block, value_block = blocks
        probs = probabilities(head_scores(query_heads, key_block), row_top, row_total).astype(
            jnp.bfloat16
        )
        return (
            carry
            + jnp.einsum("hqk,khd->qhd", probs, value_block, preferred_element_type=jnp.float32),
            None,
        )

    head_zeros = jnp.zeros((row_count, H, HD), jnp.float32)
    context, _ = lax.scan(value_step, head_zeros, (key_blocks, value_blocks))
    context_low = context.reshape(row_count, model_width).astype(jnp.bfloat16)
    attn_out = matmul(context_low, w_output) + b_output.astype(jnp.float32)
    resid_first = local_tokens.astype(jnp.float32) + attn_out
    gain_one = gain_first.astype(jnp.float32)
    shift_one = shift_first.astype(jnp.float32)
    first_norm = normalize(resid_first, gain_one, shift_one)
    first_low = first_norm.astype(jnp.bfloat16)
    inner_act = matmul(first_low, w_up) + b_up.astype(jnp.float32)
    hidden_low = gelu_exact(inner_act).astype(jnp.bfloat16)
    resid_second = first_norm + (matmul(hidden_low, w_down) + b_down.astype(jnp.float32))
    gain_two = gain_second.astype(jnp.float32)
    shift_two = shift_second.astype(jnp.float32)
    layer_out = normalize(resid_second, gain_two, shift_two)
    backward_set = (
        lax.all_gather(shards[0], "cp", axis=0, tiled=True),
        lax.all_gather(shards[1], "cp", axis=0, tiled=True),
        lax.all_gather(shards[2], "cp", axis=0, tiled=True),
        lax.all_gather(shards[3], "cp", axis=0, tiled=True),
        lax.all_gather(shards[4], "cp", axis=0, tiled=True),
        lax.all_gather(shards[5], "cp", axis=0, tiled=True),
        lax.all_gather(shards[6], "cp", axis=0, tiled=True),
        lax.all_gather(shards[7], "cp", axis=0, tiled=True),
        lax.all_gather(shards[8], "cp", axis=0, tiled=True),
        lax.all_gather(shards[9], "cp", axis=0, tiled=True),
        lax.all_gather(shards[10], "cp", axis=0, tiled=True),
        lax.all_gather(shards[11], "cp", axis=0, tiled=True),
        lax.all_gather(shards[12], "cp", axis=0, tiled=True),
        lax.all_gather(shards[13], "cp", axis=0, tiled=True),
        lax.all_gather(shards[14], "cp", axis=0, tiled=True),
    )
    (
        back_query,
        back_qbias,
        back_key,
        back_value,
        back_vbias,
        back_output,
        back_obias,
        back_gain1,
        back_shift1,
        back_up,
        back_ubias,
        back_down,
        back_dbias,
        back_gain2,
        back_shift2,
    ) = backward_set
    _, pull_second = jax.vjp(
        normalize, resid_second, back_gain2.astype(jnp.float32), back_shift2.astype(jnp.float32)
    )
    grad_resid2, grad_gain2, grad_shift2 = pull_second(cotangent[0])
    grad_outer = grad_resid2.astype(jnp.bfloat16)
    grad_down_bias = column_sum(grad_outer)
    grad_down_weight = over_rows(hidden_low, grad_outer)
    grad_hidden = against(grad_outer, back_down)
    _, pull_gelu = jax.vjp(gelu_exact, inner_act)
    grad_inner = pull_gelu(grad_hidden)[0].astype(jnp.bfloat16)
    grad_up_bias = column_sum(grad_inner)
    grad_up_weight = over_rows(first_low, grad_inner)
    grad_first = grad_resid2 + against(grad_inner, back_up)
    _, pull_first = jax.vjp(
        normalize, resid_first, back_gain1.astype(jnp.float32), back_shift1.astype(jnp.float32)
    )
    grad_resid1, grad_gain1, grad_shift1 = pull_first(grad_first)
    grad_attn = grad_resid1.astype(jnp.bfloat16)
    grad_output_bias = column_sum(grad_attn)
    grad_output_weight = over_rows(context_low, grad_attn)
    grad_context = against(grad_attn, back_output).astype(jnp.bfloat16)
    grad_heads = grad_context.reshape(row_count, H, HD)
    row_delta = jnp.sum(grad_heads.astype(jnp.float32) * context, axis=-1).T

    def key_step(carry, blocks):
        key_block, value_block = blocks
        probs_low, grad_scores = score_grads(
            query_heads, grad_heads, key_block, value_block, row_top, row_total, row_delta
        )
        new_carry = carry + jnp.einsum(
            "hqk,khd->qhd", grad_scores, key_block, preferred_element_type=jnp.float32
        )
        key_part = jnp.einsum(
            "hqk,qhd->khd", grad_scores, query_heads, preferred_element_type=jnp.float32
        )
        value_part = jnp.einsum(
            "hqk,qhd->khd", probs_low, grad_heads, preferred_element_type=jnp.float32
        )
        joined = jnp.concatenate(
            [key_part.reshape(block_len, model_width), value_part.reshape(block_len, model_width)],
            axis=1,
        )
        return (new_carry, joined)

    grad_query_heads, key_terms = lax.scan(key_step, head_zeros, (key_blocks, value_blocks))
    key_pair = lax.psum_scatter(
        key_terms.reshape(seq_len, 2 * model_width).astype(jnp.bfloat16),
        "cp",
        scatter_dimension=0,
        tiled=True,
    ).astype(jnp.float32)
    grad_key_rows = key_pair[:, :model_width]
    grad_value_rows = key_pair[:, model_width:]
    grad_query_low = grad_query_heads.reshape(row_count, model_width).astype(jnp.bfloat16)
    grad_key_low = grad_key_rows.astype(jnp.bfloat16)
    grad_value_low = grad_value_rows.astype(jnp.bfloat16)
    grad_query_weight = over_rows(local_tokens, grad_query_low)
    grad_query_bias = column_sum(grad_query_low)
    grad_key_weight = over_rows(local_tokens, grad_key_low)
    grad_value_weight = over_rows(local_tokens, grad_value_low)
    grad_value_bias = column_sum(grad_value_low)
    grad_tokens = (
        grad_resid1
        + against(grad_query_low, back_query)
        + against(grad_key_low, back_key)
        + against(grad_value_low, back_value)
    )
    input_sq = jnp.sum(grad_tokens * grad_tokens)
    grads = (
        grad_query_weight,
        grad_query_bias,
        grad_key_weight,
        grad_value_weight,
        grad_value_bias,
        grad_output_weight,
        grad_output_bias,
        grad_gain1,
        grad_shift1,
        grad_up_weight,
        grad_up_bias,
        grad_down_weight,
        grad_down_bias,
        grad_gain2,
        grad_shift2,
    )
    summed = (
        lax.psum_scatter(
            grads[0].astype(jnp.bfloat16), "cp", scatter_dimension=0, tiled=True
        ).astype(jnp.float32),
        lax.psum_scatter(
            grads[1].astype(jnp.bfloat16), "cp", scatter_dimension=0, tiled=True
        ).astype(jnp.float32),
        lax.psum_scatter(
            grads[2].astype(jnp.bfloat16), "cp", scatter_dimension=0, tiled=True
        ).astype(jnp.float32),
        lax.psum_scatter(
            grads[3].astype(jnp.bfloat16), "cp", scatter_dimension=0, tiled=True
        ).astype(jnp.float32),
        lax.psum_scatter(
            grads[4].astype(jnp.bfloat16), "cp", scatter_dimension=0, tiled=True
        ).astype(jnp.float32),
        lax.psum_scatter(
            grads[5].astype(jnp.bfloat16), "cp", scatter_dimension=0, tiled=True
        ).astype(jnp.float32),
        lax.psum_scatter(
            grads[6].astype(jnp.bfloat16), "cp", scatter_dimension=0, tiled=True
        ).astype(jnp.float32),
        lax.psum_scatter(
            grads[7].astype(jnp.bfloat16), "cp", scatter_dimension=0, tiled=True
        ).astype(jnp.float32),
        lax.psum_scatter(
            grads[8].astype(jnp.bfloat16), "cp", scatter_dimension=0, tiled=True
        ).astype(jnp.float32),
        lax.psum_scatter(
            grads[9].astype(jnp.bfloat16), "cp", scatter_dimension=0, tiled=True
        ).astype(jnp.float32),
        lax.psum_scatter(
            grads[10].astype(jnp.bfloat16), "cp", scatter_dimension=0, tiled=True
        ).astype(jnp.float32),
        lax.psum_scatter(
            grads[11].astype(jnp.bfloat16), "cp", scatter_dimension=0, tiled=True
        ).astype(jnp.float32),
        lax.psum_scatter(
            grads[12].astype(jnp.bfloat16), "cp", scatter_dimension=0, tiled=True
        ).astype(jnp.float32),
        lax.psum_scatter(
            grads[13].astype(jnp.bfloat16), "cp", scatter_dimension=0, tiled=True
        ).astype(jnp.float32),
        lax.psum_scatter(
            grads[14].astype(jnp.bfloat16), "cp", scatter_dimension=0, tiled=True
        ).astype(jnp.float32),
    )
    carried = ()
    reduced = jax.tree.map(
        lambda part: part.astype(jnp.float32), lax.psum(for_sending(tuple(summed) + carried), "rep")
    )
    input_total = lax.psum(input_sq, ("rep", "cp"))
    count_entries = lax.axis_size("rep") * lax.axis_size("cp") * row_count * model_width
    rms_values = jnp.sqrt(jnp.stack([input_total / count_entries]))
    return (
        layer_out[None],
        grad_tokens[None],
        reduced[0],
        reduced[1],
        reduced[2],
        reduced[3],
        reduced[4],
        reduced[5],
        reduced[6],
        reduced[7],
        reduced[8],
        reduced[9],
        reduced[10],
        reduced[11],
        reduced[12],
        reduced[13],
        reduced[14],
        rms_values,
    )


def solution(mesh):
    in_specs = (
        P("rep", "cp", None),
        P("cp", None),
        P("cp"),
        P("cp", None),
        P("cp", None),
        P("cp"),
        P("cp", None),
        P("cp"),
        P("cp"),
        P("cp"),
        P("cp", None),
        P("cp"),
        P("cp", None),
        P("cp"),
        P("cp"),
        P("cp"),
        P("rep", "cp", None),
    )
    out_specs = (
        P("rep", "cp", None),
        P("rep", "cp", None),
        P("cp", None),
        P("cp"),
        P("cp", None),
        P("cp", None),
        P("cp"),
        P("cp", None),
        P("cp"),
        P("cp"),
        P("cp"),
        P("cp", None),
        P("cp"),
        P("cp", None),
        P("cp"),
        P("cp"),
        P("cp"),
        P(),
    )
    return jax.shard_map(
        on_device, mesh=mesh, in_specs=in_specs, out_specs=out_specs, check_vma=False
    )
```

profile of v0, /device:TPU:0, one launch (start us, length us, event | category | flops | bytes accessed | tf_op | source)
XLA Modules:
  0.0 778.3 jit_solution(13814633855772910897)
XLA Ops:
  17.3 30.8 %all-reduce.18 = (bf16[768]{0:T(1024)(128)(2,1)S(1)}, bf16[768]{0:T(1024)(128)(2,1)S(1)}, bf16[768]{0:T(1024)(128)(2,1)S(1)}, bf16[768]{0:T(1024)(128)(2,1)S(1)}...) all-reduce(bf16[768]{0:T(1024)(128)(2,1)S(1)} %dynamic-update-slice, ...), channel_id=1, replica_groups=mesh['rep'=4,'cp'=8] {'cp'}, use_global_device_ids=true, to_apply=%add.1 | all-reduce | flops 5376 | bytes 21504
  48.1 2.6 fusion.38
  50.8 8.6 %all-gather.14.cloned.1.call-done = bf16[768,768]{1,0:T(8,128)(2,1)} async-done(((bf16[96,768]{1,0:T(8,128)(2,1)}), bf16[768,768]{1,0:T(8,128)(2,1)}) %all-gather.14.cloned.1.call-update) | async-done | bytes 1179664 | tf_op jit(solution)/shard_map/all_gather | solution.py:104
  59.5 2.5 convolution_convert_fusion.7
  67.2 12.8 %all-gather = bf16[8,1,384]{2,1,0:T(2,128)(2,1)S(1)} all-gather(bf16[1,1,384]{2,1,0:T(2,128)(2,1)S(1)} %reshape.166), channel_id=1, replica_groups=mesh['rep'=4,'cp'=8] {'cp'}, dimensions={0}, use_global_device_ids=true | all-gather | bytes 6912 | tf_op jit(solution)/shard_map/all_gather | solution.py:112
  80.5 3.1 all-gather.18.cloned.1.call-done
  83.6 1.7 fusion.39
  85.5 38.1 %all-gather.12.cloned.1.call-done = bf16[2048,768]{1,0:T(8,128)(2,1)} async-done(((bf16[256,768]{1,0:T(8,128)(2,1)}), bf16[2048,768]{1,0:T(8,128)(2,1)}) %all-gather.12.cloned.1.call-update) | async-done | bytes 3145744 | tf_op jit(solution)/shard_map/all_gather | solution.py:143
  123.6 3.2 copy.60
  126.8 4.0 reshape.138
  130.8 4.5 copy.64
  135.2 27.6 %all-gather.16.cloned.1.call-done = bf16[2048,768]{1,0:T(8,128)(2,1)} async-done(((bf16[256,768]{1,0:T(8,128)(2,1)}), bf16[2048,768]{1,0:T(8,128)(2,1)}) %all-gather.16.cloned.1.call-update) | async-done | bytes 3145744 | tf_op jit(solution)/shard_map/all_gather | solution.py:142
  162.8 3.2 copy.61
  166.0 4.0 reshape.139
  170.0 2.7 copy.65
  172.7 13.2 %while.37 = (s32[]{:T(128)}, f32[12,256]{1,0:T(8,128)S(1)}, f32[12,256]{1,0:T(8,128)}, bf16[4,512,12,64]{1,3,2,0:T(8,128)(2,1)S(1)}, bf16[256,12,64]{0,2,1:T(8,128)(2,1)S(1)}, /*index=5*/s32[]{:T(128)}, s32[]{:T(128)}) while((s32[]{:T(128)}, f32[12,256]{1,0:T(8,128)S(1)}, f32[12,256]{1,0:T(8,128)}, ...), condition=%wide.region_3.4_spmd.clone, body=%wide.region_0.3_spmd.clone.sunk | while | flops 209206272 | bytes 13922404 | solution.py:162
  185.9 16.7 %while.38 = (s32[]{:T(128)}, f32[256,12,64]{0,2,1:T(8,128)}, bf16[4,512,12,64]{1,3,2,0:T(8,128)(2,1)}, bf16[4,512,12,64]{1,3,2,0:T(8,128)(2,1)S(1)}, bf16[256,12...) while((s32[]{:T(128)}, f32[256,12,64]{0,2,1:T(8,128)}, ...), condition=%wide.region_5.6_spmd.clone, body=%wide.region_4.5_spmd.clone.sunk | while | flops 409337856 | bytes 3573358 | solution.py:176
  185.9 3.9 fusion.124
  189.8 4.2 fusion.124
  194.0 4.3 fusion.124
  198.4 4.2 fusion.124
  202.6 2.5 convert_element_type.222
  205.1 2.9 fusion.63
  211.0 27.6 %all-gather.22.cloned.1.call-done = bf16[768,3072]{1,0:T(8,128)(2,1)} async-done(((bf16[96,3072]{1,0:T(8,128)(2,1)}), bf16[768,3072]{1,0:T(8,128)(2,1)}) %all-gather.22.cloned.1.call-update) | async-done | bytes 4718608 | tf_op jit(solution)/shard_map/all_gather | solution.py:111
  238.6 6.6 multiply_convert_fusion.1
  245.1 45.1 %all-gather.24.cloned.1.call-done = bf16[3072,768]{1,0:T(8,128)(2,1)} async-done(((bf16[384,768]{1,0:T(8,128)(2,1)}), bf16[3072,768]{1,0:T(8,128)(2,1)}) %all-gather.24.cloned.1.call-update) | async-done | bytes 4718608 | tf_op jit(solution)/shard_map/all_gather | solution.py:113
  290.2 4.7 fusion.64
  297.2 3.6 fusion.57
  300.8 4.0 multiply_reduce_fusion.1
  309.3 46.7 %while.39 = (s32[]{:T(128)}, f32[256,12,64]{0,2,1:T(8,128)S(1)}, bf16[4,512,1536]{2,1,0:T(8,128)(2,1)}, bf16[4,512,12,64]{1,3,2,0:T(8,128)(2,1)}, bf16[256,12,64...) while((s32[]{:T(128)}, f32[256,12,64]{0,2,1:T(8,128)S(1)}, ...), condition=%wide.region_16.17_spmd.clone, body=%wide.region_15.16_spmd.clone.sunk | while | flops 1022754816 | bytes 54309124 | solution.py:268
  309.3 2.7 exponential_divide_fusion.2
  313.1 2.3 multiply_convert_fusion.3
  315.5 1.8 fusion.135
  321.0 2.7 exponential_divide_fusion.2
  324.8 2.3 multiply_convert_fusion.3
  327.2 1.8 fusion.135
  332.7 2.7 exponential_divide_fusion.2
  336.5 2.3 multiply_convert_fusion.3
  338.8 1.8 fusion.135
  344.4 2.7 exponential_divide_fusion.2
  348.2 2.3 multiply_convert_fusion.3
  350.5 1.8 fusion.135
  359.1 65.7 %reduce-scatter.14.cloned.1.call-done = bf16[256,1536]{1,0:T(8,128)(2,1)} async-done(((bf16[2048,1536]{1,0:T(8,128)(2,1)}), bf16[256,1536]{1,0:T(8,128)(2,1)}) %reduce-scatter.14.cloned.1.call-update) | async-done | bytes 786448 | tf_op jit(solution)/shard_map/reduce_scatter | solution.py:269
  431.9 4.9 convolution_convert_fusion.1
  438.2 3.6 convolution_convert_fusion
  441.9 16.9 %reduce-scatter.22.cloned.1.call-done = bf16[96,768]{1,0:T(8,128)(2,1)} async-done(((bf16[768,768]{1,0:T(8,128)(2,1)}), bf16[96,768]{1,0:T(8,128)(2,1)}) %reduce-scatter.22.cloned.1.call-update) | async-done | bytes 147472
  458.9 1.7 copy.74
  460.6 31.8 %reduce-scatter.26.cloned.1.call-done = bf16[96,768]{1,0:T(8,128)(2,1)} async-done(((bf16[768,768]{1,0:T(8,128)(2,1)}), bf16[96,768]{1,0:T(8,128)(2,1)}) %reduce-scatter.26.cloned.1.call-update) | async-done | bytes 147472
  492.4 1.7 copy.78
  494.1 32.0 %reduce-scatter.24.cloned.1.call-done = bf16[96,768]{1,0:T(8,128)(2,1)} async-done(((bf16[768,768]{1,0:T(8,128)(2,1)}), bf16[96,768]{1,0:T(8,128)(2,1)}) %reduce-scatter.24.cloned.1.call-update) | async-done | bytes 147472
  526.1 1.7 copy.76
  527.8 31.8 %reduce-scatter.16.cloned.1.call-done = bf16[96,768]{1,0:T(8,128)(2,1)} async-done(((bf16[768,768]{1,0:T(8,128)(2,1)}), bf16[96,768]{1,0:T(8,128)(2,1)}) %reduce-scatter.16.cloned.1.call-update) | async-done | bytes 147472 | tf_op jit(solution)/shard_map/reduce_scatter | solution.py:325
  559.6 55.3 %reduce-scatter.18.cloned.1.call-done = bf16[96,3072]{1,0:T(8,128)(2,1)} async-done(((bf16[768,3072]{1,0:T(8,128)(2,1)}), bf16[96,3072]{1,0:T(8,128)(2,1)}) %reduce-scatter.18.cloned.1.call-update) | async-done | bytes 589840 | tf_op jit(solution)/shard_map/reduce_scatter | solution.py:337
  614.9 55.5 %reduce-scatter.20.cloned.1.call-done = bf16[384,768]{1,0:T(8,128)(2,1)} async-done(((bf16[3072,768]{1,0:T(8,128)(2,1)}), bf16[384,768]{1,0:T(8,128)(2,1)}) %reduce-scatter.20.cloned.1.call-update) | async-done | bytes 589840 | tf_op jit(solution)/shard_map/reduce_scatter | solution.py:343
  673.3 2.0 convolution_add_fusion.3
  676.0 2.0 multiply_reduce_fusion
  677.9 38.4 %psum.127 = f32[]{:T(128)} all-reduce(f32[]{:T(128)} %get-tuple-element.440), channel_id=1, replica_groups=mesh['rep'=4,'cp'=8] {'rep','cp'}, use_global_device_ids=true, to_apply=%region_58.59 | all-reduce | flops 1 | bytes 8 | tf_op jit(solution)/shard_map/psum | solution.py:360
  717.2 26.8 %all-reduce.17 = (bf16[768]{0:T(1024)(128)(2,1)S(1)}, bf16[768]{0:T(1024)(128)(2,1)S(1)}, bf16[768]{0:T(1024)(128)(2,1)S(1)}, bf16[768]{0:T(1024)(128)(2,1)S(1)}...) all-reduce(bf16[768]{0:T(1024)(128)(2,1)S(1)} %copy-done.53, ...), channel_id=1, replica_groups=mesh['rep'=4,'cp'=8] {'cp'}, use_global_device_ids=true, to_apply=%add.7 | all-reduce | flops 9984 | bytes 39936
  744.7 9.9 %all-reduce.19 = (bf16[96]{0:T(256)(128)(2,1)S(1)}, bf16[96]{0:T(256)(128)(2,1)S(1)}, bf16[96]{0:T(256)(128)(2,1)S(1)}, bf16[96]{0:T(256)(128)(2,1)S(1)}, bf16[9...) all-reduce(bf16[96]{0:T(256)(128)(2,1)S(1)} %dynamic-slice.9, ...), channel_id=1, replica_groups=mesh['rep'=4,'cp'=8] {'rep'}, use_global_device_ids=true, to_apply=%region_22.23 | all-reduce | flops 1152 | bytes 4608 | tf_op jit(solution)/shard_map/psum | solution.py:358
  760.4 1.8 copy.70
  762.2 1.8 copy.71
  763.9 1.8 copy.72
  765.7 1.6 convert_element_type.254
  767.4 2.2 convert_element_type.261
  (312 shorter events, 78.2 us)
Async XLA Ops:
  7.2 52.3 %copy-start.8 = (bf16[1,256,768]{2,1,0:T(8,128)(2,1)S(1)}, bf16[1,256,768]{2,1,0:T(8,128)(2,1)}, u32[]{:S(2)}) copy-start(bf16[1,256,768]{2,1,0:T(8,128)(2,1)} %param.23) | copy-start | bytes 1179652
  7.2 40.9 %all-gather.10.cloned.1.call-start = ((), (), s32[]{:S(2)}) async-start(), calls=%async_computation.7 | async-start | bytes 1327104 | tf_op jit(solution)/shard_map/all_gather | solution.py:105
  7.9 51.5 %all-gather.14.cloned.1.call-start = ((), (), s32[]{:S(2)}) async-start(), calls=%async_computation.9 | async-start | bytes 1327104 | tf_op jit(solution)/shard_map/all_gather | solution.py:104
  8.7 74.9 %all-gather.18.cloned.1.call-start = ((), (), s32[]{:S(2)}) async-start(), calls=%async_computation.11 | async-start | bytes 1327104 | tf_op jit(solution)/shard_map/all_gather | solution.py:102
  9.4 114.2 %all-gather.12.cloned.1.call-start = ((), (), s32[]{:S(2)}) async-start(), calls=%async_computation.8 | async-start | bytes 3538944 | tf_op jit(solution)/shard_map/all_gather | solution.py:143
  48.1 16.0 %copy-start.57 = (bf16[384]{0:T(512)(128)(2,1)S(1)}, bf16[384]{0:T(512)(128)(2,1)}, u32[]{:S(2)}) copy-start(bf16[384]{0:T(512)(128)(2,1)} %param.34) | copy-start | bytes 2308
  50.8 112.0 %all-gather.16.cloned.1.call-start = ((), (), s32[]{:S(2)}) async-start(), calls=%async_computation.10 | async-start | bytes 3538944 | tf_op jit(solution)/shard_map/all_gather | solution.py:142
  62.0 143.1 %all-gather.20.cloned.1.call-start = ((), (), s32[]{:S(2)}) async-start(), calls=%async_computation.12 | async-start | bytes 1327104 | tf_op jit(solution)/shard_map/all_gather | solution.py:107
  62.6 176.0 %all-gather.22.cloned.1.call-start = ((), (), s32[]{:S(2)}) async-start(), calls=%async_computation.13 | async-start | bytes 5308416 | tf_op jit(solution)/shard_map/all_gather | solution.py:111
  63.3 226.9 %all-gather.24.cloned.1.call-start = ((), (), s32[]{:S(2)}) async-start(), calls=%async_computation.14 | async-start | bytes 5308416 | tf_op jit(solution)/shard_map/all_gather | solution.py:113
  64.1 360.7 %reduce-scatter.14.cloned.1.call-start = ((), (), s32[]{:S(2)}) async-start(), calls=%async_computation.15 | async-start | bytes 7077888 | tf_op jit(solution)/shard_map/reduce_scatter | solution.py:269
  202.6 92.3 %copy-start.2 = (bf16[4,512,12,64]{1,3,2,0:T(8,128)(2,1)}, bf16[4,512,12,64]{1,3,2,0:T(8,128)(2,1)S(1)}, u32[]{:S(2)}) copy-start(bf16[4,512,12,64]{1,3,2,0:T(8,128)(2,1)S(1)} %get-tuple-element.695) | copy-start | bytes 9437188
  290.2 6.9 slice-start.2
  290.2 4.9 copy-start.10
  290.2 5.0 copy-start.32
  290.2 6.9 slice-start.3
  294.9 2.2 copy-start.59
  296.4 4.4 slice-start
  297.1 3.7 copy-start.23
  297.1 3.7 copy-start.29
  297.1 3.7 copy-start.37
  297.1 3.7 copy-start.41
  297.2 3.7 slice-start.1
  300.8 4.0 copy-start.25
  300.8 4.0 copy-start.44
  304.8 3.1 copy-start.16
  304.8 3.8 copy-start.22
  306.4 2.9 copy-start.3
  309.3 8.0 %copy-start = (bf16[256,12,64]{0,2,1:T(8,128)(2,1)}, bf16[256,12,64]{0,2,1:T(8,128)(2,1)S(1)}, u32[]{:S(2)}) copy-start(bf16[256,12,64]{0,2,1:T(8,128)(2,1)S(1)} %get-tuple-element.657) | copy-start | bytes 1179652 | tf_op jit(solution)/shard_map/while
  321.0 8.0 %copy-start = (bf16[256,12,64]{0,2,1:T(8,128)(2,1)}, bf16[256,12,64]{0,2,1:T(8,128)(2,1)S(1)}, u32[]{:S(2)}) copy-start(bf16[256,12,64]{0,2,1:T(8,128)(2,1)S(1)} %get-tuple-element.657) | copy-start | bytes 1179652 | tf_op jit(solution)/shard_map/while
  332.7 8.0 %copy-start = (bf16[256,12,64]{0,2,1:T(8,128)(2,1)}, bf16[256,12,64]{0,2,1:T(8,128)(2,1)S(1)}, u32[]{:S(2)}) copy-start(bf16[256,12,64]{0,2,1:T(8,128)(2,1)S(1)} %get-tuple-element.657) | copy-start | bytes 1179652 | tf_op jit(solution)/shard_map/while
  344.4 8.0 %copy-start = (bf16[256,12,64]{0,2,1:T(8,128)(2,1)}, bf16[256,12,64]{0,2,1:T(8,128)(2,1)S(1)}, u32[]{:S(2)}) copy-start(bf16[256,12,64]{0,2,1:T(8,128)(2,1)S(1)} %get-tuple-element.657) | copy-start | bytes 1179652 | tf_op jit(solution)/shard_map/while
  356.1 102.8 %reduce-scatter.22.cloned.1.call-start = ((), (), s32[]{:S(2)}) async-start(), calls=%async_computation.19 | async-start | bytes 1327104
  359.0 133.4 %reduce-scatter.26.cloned.1.call-start = ((), (), s32[]{:S(2)}) async-start(), calls=%async_computation.21 | async-start | bytes 1327104
  424.7 3.2 copy-start.14
  427.9 98.3 %reduce-scatter.24.cloned.1.call-start = ((), (), s32[]{:S(2)}) async-start(), calls=%async_computation.20 | async-start | bytes 1327104
  428.4 3.4 copy-start.30
  428.5 3.4 copy-start.31
  428.5 3.4 copy-start.38
  428.5 3.4 copy-start.42
  430.0 129.7 %reduce-scatter.16.cloned.1.call-start = ((), (), s32[]{:S(2)}) async-start(), calls=%async_computation.16 | async-start | bytes 1327104 | tf_op jit(solution)/shard_map/reduce_scatter | solution.py:325
  431.5 183.4 %reduce-scatter.18.cloned.1.call-start = ((), (), s32[]{:S(2)}) async-start(), calls=%async_computation.17 | async-start | bytes 5308416 | tf_op jit(solution)/shard_map/reduce_scatter | solution.py:337
  436.8 233.7 %reduce-scatter.20.cloned.1.call-start = ((), (), s32[]{:S(2)}) async-start(), calls=%async_computation.18 | async-start | bytes 5308416 | tf_op jit(solution)/shard_map/reduce_scatter | solution.py:343
  441.9 229.9 %copy-start.11 = (f32[1,256,768]{2,1,0:T(8,128)S(1)}, f32[1,256,768]{2,1,0:T(8,128)}, u32[]{:S(2)}) copy-start(f32[1,256,768]{2,1,0:T(8,128)} %param.39) | copy-start | bytes 2359300
  441.9 230.6 %copy-start.58 = (bf16[96]{0:T(256)(128)(2,1)S(1)}, bf16[96]{0:T(256)(128)(2,1)}, u32[]{:S(2)}) copy-start(bf16[96]{0:T(256)(128)(2,1)} %param.38) | copy-start | bytes 580
  441.9 231.4 %copy-start.13 = (f32[256,768]{1,0:T(8,128)S(1)}, f32[256,768]{1,0:T(8,128)}, u32[]{:S(2)}) copy-start(f32[256,768]{1,0:T(8,128)} %copy-done.12) | copy-start | bytes 2359300
  441.9 231.4 %copy-start.46 = (f32[256]{0:T(256)S(1)}, f32[256]{0:T(256)}, u32[]{:S(2)}) copy-start(f32[256]{0:T(256)} %copy-done.45) | copy-start | bytes 3076
  441.9 318.4 %all-reduce.23.cloned.1.call-start = ((), (), s32[]{:S(2)}) async-start(), calls=%async_computation.22 | async-start | bytes 3833856 | tf_op jit(solution)/shard_map/psum | solution.py:358
  494.1 181.2 %copy-start.15 = (bf16[768,768]{1,0:T(8,128)(2,1)S(1)}, bf16[768,768]{1,0:T(8,128)(2,1)}, u32[]{:S(2)}) copy-start(bf16[768,768]{1,0:T(8,128)(2,1)} %all-gather.14.cloned.1.call-done) | copy-start | bytes 3538948
  673.3 2.6 copy-start.27
  675.3 41.8 %copy-start.47 = (bf16[768]{0:T(1024)(128)(2,1)S(1)}, bf16[768]{0:T(1024)(128)(2,1)}, u32[]{:S(2)}) copy-start(bf16[768]{0:T(1024)(128)(2,1)} %get-tuple-element.336) | copy-start | bytes 4612
  675.3 83.9 %copy-start.7 = (f32[256,768]{1,0:T(8,128)S(1)}, f32[256,768]{1,0:T(8,128)}, u32[]{:S(2)}) copy-start(f32[256,768]{1,0:T(8,128)} %copy-done.6) | copy-start | bytes 2359300
  675.3 83.9 %copy-start.33 = (f32[768]{0:T(1024)S(1)}, f32[768]{0:T(1024)}, u32[]{:S(2)}) copy-start(f32[768]{0:T(1024)} %convert_element_type.231) | copy-start | bytes 9220
  675.3 83.9 %copy-start.35 = (f32[256]{0:T(256)S(1)}, f32[256]{0:T(256)}, u32[]{:S(2)}) copy-start(f32[256]{0:T(256)} %copy-done.34) | copy-start | bytes 3076
  675.3 83.9 %copy-start.40 = (f32[256]{0:T(256)S(1)}, f32[256]{0:T(256)}, u32[]{:S(2)}) copy-start(f32[256]{0:T(256)} %copy-done.39) | copy-start | bytes 3076
  675.9 41.3 %copy-start.48 = (bf16[768]{0:T(1024)(128)(2,1)S(1)}, bf16[768]{0:T(1024)(128)(2,1)}, u32[]{:S(2)}) copy-start(bf16[768]{0:T(1024)(128)(2,1)} %get-tuple-element.417) | copy-start | bytes 4612
  675.9 41.3 %copy-start.49 = (bf16[768]{0:T(1024)(128)(2,1)S(1)}, bf16[768]{0:T(1024)(128)(2,1)}, u32[]{:S(2)}) copy-start(bf16[768]{0:T(1024)(128)(2,1)} %get-tuple-element.421) | copy-start | bytes 4612
  675.9 41.3 %copy-start.50 = (bf16[768]{0:T(1024)(128)(2,1)S(1)}, bf16[768]{0:T(1024)(128)(2,1)}, u32[]{:S(2)}) copy-start(bf16[768]{0:T(1024)(128)(2,1)} %reduce_sum.263) | copy-start | bytes 4612
  675.9 41.3 %copy-start.51 = (bf16[768]{0:T(1024)(128)(2,1)S(1)}, bf16[768]{0:T(1024)(128)(2,1)}, u32[]{:S(2)}) copy-start(bf16[768]{0:T(1024)(128)(2,1)} %reduce_sum.224) | copy-start | bytes 4612
  675.9 41.3 %copy-start.53 = (bf16[768]{0:T(1024)(128)(2,1)S(1)}, bf16[768]{0:T(1024)(128)(2,1)}, u32[]{:S(2)}) copy-start(bf16[768]{0:T(1024)(128)(2,1)} %copy-done.52) | copy-start | bytes 4612
  675.9 41.3 %copy-start.54 = (bf16[3072]{0:T(1024)(128)(2,1)S(1)}, bf16[3072]{0:T(1024)(128)(2,1)}, u32[]{:S(2)}) copy-start(bf16[3072]{0:T(1024)(128)(2,1)} %get-tuple-element.419) | copy-start | bytes 18436
  675.9 41.3 %copy-start.55 = (bf16[768]{0:T(1024)(128)(2,1)S(1)}, bf16[768]{0:T(1024)(128)(2,1)}, u32[]{:S(2)}) copy-start(bf16[768]{0:T(1024)(128)(2,1)} %get-tuple-element.338) | copy-start | bytes 4612
  675.9 41.3 %copy-start.56 = (bf16[768]{0:T(1024)(128)(2,1)S(1)}, bf16[768]{0:T(1024)(128)(2,1)}, u32[]{:S(2)}) copy-start(bf16[768]{0:T(1024)(128)(2,1)} %get-tuple-element.340) | copy-start | bytes 4612
  760.3 9.2 %copy-start.28 = (bf16[384,768]{1,0:T(8,128)(2,1)S(1)}, bf16[384,768]{1,0:T(8,128)(2,1)}, u32[]{:S(2)}) copy-start(bf16[384,768]{1,0:T(8,128)(2,1)} %get-tuple-element.416) | copy-start | bytes 1769476
  (28 other events, 35.7 us)
Sparse Core Ops, SparseCore 0:
  9.6 25.6 all-gather.9
  36.9 22.4 all-gather.13
  61.1 22.4 all-gather.17
  85.7 37.8 all-gather.11
  125.7 37.1 all-gather.15
  164.3 21.6 all-gather.19
  187.7 50.8 all-gather.21
  240.2 49.9 all-gather.23
  356.2 68.4 reduce-scatter.13
  427.4 31.3 reduce-scatter.21
  461.2 31.1 reduce-scatter.25
  495.1 30.9 reduce-scatter.23
  528.4 31.1 reduce-scatter.15
  561.8 53.0 reduce-scatter.17
  617.1 53.3 reduce-scatter.19
  674.7 66.5 all-reduce.22
where the time goes:
time: 780 us; the launch traced here: 778 us
  waiting for transfers between devices  443 us (57%)
  blocking collectives  119 us (15%)
  matrix products  103 us (13%)
  local copies, waits for them, and re-layouts  59.7 us (8%)
  other arithmetic  34 us (4%)
  between operations  18.6 us (2%)
    unnamed x19, waiting for transfers between devices  84.9 us
    reduce_scatter x1, waiting for transfers between devices, on_device(): lax.psum_scatter(key_terms.reshape(seq_len, 2 * model_width).astype(jnp.b...  65.7 us
    unnamed x2, blocking collectives  57.6 us
    reduce_scatter x1, waiting for transfers between devices, on_device(): lax.psum_scatter(grads[11].astype(jnp.bfloat16), 'cp', scatter_dimension=...  55.5 us
    reduce_scatter x1, waiting for transfers between devices, on_device(): lax.psum_scatter(grads[9].astype(jnp.bfloat16), 'cp', scatter_dimension=0...  55.3 us
    all_gather x1, waiting for transfers between devices, on_device(): lax.all_gather(shards[11], 'cp', axis=0, tiled=True)  45.1 us
    psum x1, blocking collectives, on_device(): input_total = lax.psum(input_sq, ('rep', 'cp'))  38.4 us
    all_gather x1, waiting for transfers between devices, on_device(): lax.all_gather(value_rows, 'cp', axis=0, tiled=True)  38.1 us
  transfers between devices with their start and end apart: 16, of which 13 were waited for; matrix products, arithmetic and copies ran while one was open for 15% of the time, Pallas kernels for 0%

commit v1 on v0

--- a/solution.py
+++ b/solution.py
@@ -3,6 +3,7 @@
 import jax.numpy as jnp
 from jax import lax
 from jax.sharding import PartitionSpec as P
+from jax.lax import axis_index, axis_size, ppermute
 
 H = 12
 HD = 64
@@ -81,6 +82,20 @@
     second_shift,
     cotangent,
 ):
+
+    def bind_body(in_array):
+        width = axis_size("cp")
+        table = [in_array]
+        for i0 in range(1, width):
+            built = ppermute(
+                table[i0 - 1], "cp", [(dev_j, (dev_j - 1) % width) for dev_j in range(width)]
+            )
+            table.append(built)
+        current_arr = jnp.concatenate(table, 0)
+        b_now = axis_index("cp")
+        f_next = jnp.roll(current_arr, b_now * in_array.shape[0], 0)
+        return f_next
+
     shards = (
         query_weight,
         query_bias,
@@ -139,7 +154,7 @@
     key_rows = matmul(local_tokens, w_key).astype(jnp.bfloat16)
     value_rows = (matmul(local_tokens, w_value) + b_value.astype(jnp.float32)).astype(jnp.bfloat16)
     all_keys, all_values = (
-        lax.all_gather(key_rows, "cp", axis=0, tiled=True),
+        bind_body(key_rows),
         lax.all_gather(value_rows, "cp", axis=0, tiled=True),
     )
     seq_len = all_keys.shape[0]

time: 780 us -> 776 us (level)
  waiting for transfers between devices: 443 us -> 350 us
  starting transfers between devices: 0.9 us -> 24.9 us
  matrix products: 103 us -> 126 us
  local copies, waits for them, and re-layouts: 59.7 us -> 81.8 us
  other arithmetic: 34 us -> 48 us
    ppermute x0 -> x7, waiting for transfers between devices: none -> 42.6 us  [bind_body(): ppermute(table[i0 - 1], 'cp', [(dev_j, (dev_j - 1) % width) for dev_j in...]
    all_gather x1, waiting for transfers between devices: 38.1 us -> 0.01 us  [on_device(): lax.all_gather(value_rows, 'cp', axis=0, tiled=True)]
    all_gather x1, waiting for transfers between devices: 45.1 us -> 9.69 us  [on_device(): lax.all_gather(shards[11], 'cp', axis=0, tiled=True)]
    all_gather x1 -> x0, waiting for transfers between devices: 27.6 us -> none  [on_device(): lax.all_gather(key_rows, 'cp', axis=0, tiled=True)]
    all_gather x1, waiting for transfers between devices: 27.6 us -> 0.02 us  [on_device(): lax.all_gather(shards[9], 'cp', axis=0, tiled=True)]
    ppermute x0 -> x7, starting transfers between devices: none -> 24 us  [bind_body(): ppermute(table[i0 - 1], 'cp', [(dev_j, (dev_j - 1) % width) for dev_j in...]
    dot_general x8, matrix products: 15.1 us -> 30.4 us  [head_scores(): jnp.einsum('qhd,khd->hqk', query_heads, key_heads, preferred_element_type...]
    dynamic_update_slice x8, local copies, waits for them, and re-layouts: 7.96 us -> 21.1 us  [on_device(): lax.scan(key_step, head_zeros, (key_blocks, value_blocks))]
  transfers between devices with their start and end apart: 16 -> 22, of which waited for: 13 -> 15; matrix products, arithmetic and copies ran while one was open for 15% -> 20% of each run, Pallas kernels for 0% -> 0%
where the time goes in v1:
time: 776 us; the launch traced here: 773 us
  waiting for transfers between devices  350 us (45%)
  matrix products  126 us (16%)
  blocking collectives  124 us (16%)
  local copies, waits for them, and re-layouts  81.8 us (11%)
  other arithmetic  48 us (6%)
  starting transfers between devices  24.9 us (3%)
  between operations  18.6 us (2%)
    unnamed x18, waiting for transfers between devices  83 us
    reduce_scatter x1, waiting for transfers between devices, on_device(): lax.psum_scatter(key_terms.reshape(seq_len, 2 * model_width).astype(jnp.b...  64.6 us
    unnamed x2, blocking collectives  57.6 us
    reduce_scatter x1, waiting for transfers between devices, on_device(): lax.psum_scatter(grads[9].astype(jnp.bfloat16), 'cp', scatter_dimension=0...  55.5 us
    reduce_scatter x1, waiting for transfers between devices, on_device(): lax.psum_scatter(grads[11].astype(jnp.bfloat16), 'cp', scatter_dimension=...  55.4 us
    ppermute x7, waiting for transfers between devices, bind_body(): ppermute(table[i0 - 1], 'cp', [(dev_j, (dev_j - 1) % width) for dev_j in...  42.6 us
    unnamed x178, local copies, waits for them, and re-layouts  41 us
    psum x1, blocking collectives, on_device(): input_total = lax.psum(input_sq, ('rep', 'cp'))  38.4 us
  transfers between devices with their start and end apart: 22, of which 15 were waited for; matrix products, arithmetic and copies ran while one was open for 20% of the time, Pallas kernels for 0%

profile of v1, /device:TPU:0, one launch (start us, length us, event | category | flops | bytes accessed | tf_op | source)
XLA Modules:
  0.0 773.3 jit_solution(4608198820472222871)
XLA Ops:
  17.3 30.8 %all-reduce.18 = (bf16[768]{0:T(1024)(128)(2,1)S(1)}, bf16[768]{0:T(1024)(128)(2,1)S(1)}, bf16[768]{0:T(1024)(128)(2,1)S(1)}, bf16[768]{0:T(1024)(128)(2,1)S(1)}...) all-reduce(bf16[768]{0:T(1024)(128)(2,1)S(1)} %dynamic-update-slice, ...), channel_id=1, replica_groups=mesh['rep'=4,'cp'=8] {'cp'}, use_global_device_ids=true, to_apply=%add.1 | all-reduce | flops 5376 | bytes 21504
  48.2 2.6 fusion.38
  52.0 7.4 all-gather.13.cloned.1.call-done
  64.0 6.4 collective-permute-done
  70.4 3.7 collective-permute-start.1
  74.2 9.2 %collective-permute-done.1 = bf16[256,768]{1,0:T(8,128)(2,1)S(1)} collective-permute-done((bf16[256,768]{1,0:T(8,128)(2,1)S(1)}, bf16[256,768]{1,0:T(8,128)(2,1)S(1)}, u32[]{:S(2)}, u32[]{:S(2)}) %collective-permute-start.1) | collective-permute-done | bytes 393248 | tf_op jit(solution)/shard_map/ppermute | solution.py:90
  83.4 3.7 collective-permute-start.2
  87.1 5.3 collective-permute-done.2
  92.4 3.7 collective-permute-start.3
  96.1 13.6 %collective-permute-done.3 = bf16[256,768]{1,0:T(8,128)(2,1)S(1)} collective-permute-done((bf16[256,768]{1,0:T(8,128)(2,1)S(1)}, bf16[256,768]{1,0:T(8,128)(2,1)S(1)}, u32[]{:S(2)}, u32[]{:S(2)}) %collective-permute-start.3) | collective-permute-done | bytes 393248 | tf_op jit(solution)/shard_map/ppermute | solution.py:90
  109.7 3.8 collective-permute-start.4
  115.9 18.0 %all-gather = bf16[8,1,384]{2,1,0:T(2,128)(2,1)S(1)} all-gather(bf16[1,1,384]{2,1,0:T(2,128)(2,1)S(1)} %reshape.166), channel_id=1, replica_groups=mesh['rep'=4,'cp'=8] {'cp'}, dimensions={0}, use_global_device_ids=true | all-gather | bytes 6912 | tf_op jit(solution)/shard_map/all_gather | solution.py:127
  135.7 3.3 collective-permute-start.5
  145.9 3.8 collective-permute-start.6
  152.8 5.5 collective-permute-done.6
  167.5 3.0 copy.60
  170.4 4.9 reshape.139
  177.8 39.8 %while.37 = (s32[]{:T(128)}, f32[12,256]{1,0:T(8,128)S(1)}, f32[12,256]{1,0:T(8,128)}, bf16[4,512,12,64]{1,3,2,0:T(8,128)(2,1)}, bf16[256,12,64]{0,2,1:T(8,128)(2,1)}, /*index=5*/s32[]{:T(128)}, s32[]{:T(128)}) while((s32[]{:T(128)}, f32[12,256]{1,0:T(8,128)S(1)}, f32[12,256]{1,0:T(8,128)}, bf16[4,512,12,64]{1,3,2,0:T(8,128)(2,1)}, ...), condition=%wide.region_3.4_spmd.clone, body=%wide.region_0.3_spmd.clone.sunk | while | flops 209206272 | bytes 13922904 | solution.py:177
  177.8 4.9 bitcast_reduce_fusion.2
  182.7 3.9 fusion.119
  187.2 4.9 bitcast_reduce_fusion.2
  192.1 3.9 fusion.119
  197.4 4.9 bitcast_reduce_fusion.2
  202.3 3.9 fusion.119
  207.5 4.9 bitcast_reduce_fusion.2
  212.4 3.9 fusion.119
  217.6 3.2 copy.59
  220.8 4.0 reshape.138
  224.8 2.6 copy.63
  227.4 17.1 %while.38 = (s32[]{:T(128)}, f32[256,12,64]{0,2,1:T(8,128)}, bf16[4,512,12,64]{1,3,2,0:T(8,128)(2,1)S(1)}, bf16[4,512,12,64]{1,3,2,0:T(8,128)(2,1)}, bf16[256,12...) while((s32[]{:T(128)}, f32[256,12,64]{0,2,1:T(8,128)}, ...), condition=%wide.region_5.6_spmd.clone, body=%wide.region_4.5_spmd.clone.sunk | while | flops 409337856 | bytes 3572839 | solution.py:191
  227.4 4.1 fusion.124
  231.5 4.4 fusion.124
  235.9 4.3 fusion.124
  240.2 4.4 fusion.124
  250.2 6.6 multiply_convert_fusion.1
  256.8 9.7 %all-gather.21.cloned.1.call-done = bf16[3072,768]{1,0:T(8,128)(2,1)} async-done(((bf16[384,768]{1,0:T(8,128)(2,1)}), bf16[3072,768]{1,0:T(8,128)(2,1)}) %all-gather.21.cloned.1.call-update) | async-done | bytes 4718608 | tf_op jit(solution)/shard_map/all_gather | solution.py:128
  266.6 4.6 fusion.64
  273.6 3.6 fusion.57
  282.8 70.2 %while.39 = (s32[]{:T(128)}, f32[256,12,64]{0,2,1:T(8,128)}, bf16[4,512,1536]{2,1,0:T(8,128)(2,1)}, bf16[4,512,12,64]{1,3,2,0:T(8,128)(2,1)}, bf16[256,12,64]{0,...) while((s32[]{:T(128)}, f32[256,12,64]{0,2,1:T(8,128)}, ...), condition=%wide.region_16.17_spmd.clone, body=%wide.region_15.16_spmd.clone.sunk | while | flops 1022754816 | bytes 44918936 | solution.py:283
  282.8 2.7 exponential_divide_fusion.2
  294.8 2.7 constant_dynamic-update-slice_fusion.18
  297.5 2.6 fusion.135
  300.1 2.7 exponential_divide_fusion.2
  309.6 2.6 copy.95
  312.2 2.7 constant_dynamic-update-slice_fusion.18
  314.8 2.9 fusion.135
  317.7 2.7 exponential_divide_fusion.2
  329.8 2.8 constant_dynamic-update-slice_fusion.18
  332.5 2.9 fusion.135
  335.4 2.7 exponential_divide_fusion.2
  347.4 2.7 constant_dynamic-update-slice_fusion.18
  350.1 2.9 fusion.135
  357.0 64.6 %reduce-scatter.14.cloned.1.call-done = bf16[256,1536]{1,0:T(8,128)(2,1)} async-done(((bf16[2048,1536]{1,0:T(8,128)(2,1)}), bf16[256,1536]{1,0:T(8,128)(2,1)}) %reduce-scatter.14.cloned.1.call-update) | async-done | bytes 786448 | tf_op jit(solution)/shard_map/reduce_scatter | solution.py:284
  428.7 5.0 convolution_convert_fusion
  434.9 5.2 convolution_convert_fusion.1
  440.2 15.8 %reduce-scatter.22.cloned.1.call-done = bf16[96,768]{1,0:T(8,128)(2,1)} async-done(((bf16[768,768]{1,0:T(8,128)(2,1)}), bf16[96,768]{1,0:T(8,128)(2,1)}) %reduce-scatter.22.cloned.1.call-update) | async-done | bytes 147472
  457.7 32.1 %reduce-scatter.24.cloned.1.call-done = bf16[96,768]{1,0:T(8,128)(2,1)} async-done(((bf16[768,768]{1,0:T(8,128)(2,1)}), bf16[96,768]{1,0:T(8,128)(2,1)}) %reduce-scatter.24.cloned.1.call-update) | async-done | bytes 147472
  491.5 31.9 %reduce-scatter.26.cloned.1.call-done = bf16[96,768]{1,0:T(8,128)(2,1)} async-done(((bf16[768,768]{1,0:T(8,128)(2,1)}), bf16[96,768]{1,0:T(8,128)(2,1)}) %reduce-scatter.26.cloned.1.call-update) | async-done | bytes 147472
  525.1 31.8 %reduce-scatter.16.cloned.1.call-done = bf16[96,768]{1,0:T(8,128)(2,1)} async-done(((bf16[768,768]{1,0:T(8,128)(2,1)}), bf16[96,768]{1,0:T(8,128)(2,1)}) %reduce-scatter.16.cloned.1.call-update) | async-done | bytes 147472 | tf_op jit(solution)/shard_map/reduce_scatter | solution.py:340
  556.9 55.4 %reduce-scatter.20.cloned.1.call-done = bf16[384,768]{1,0:T(8,128)(2,1)} async-done(((bf16[3072,768]{1,0:T(8,128)(2,1)}), bf16[384,768]{1,0:T(8,128)(2,1)}) %reduce-scatter.20.cloned.1.call-update) | async-done | bytes 589840 | tf_op jit(solution)/shard_map/reduce_scatter | solution.py:358
  612.3 55.5 %reduce-scatter.18.cloned.1.call-done = bf16[96,3072]{1,0:T(8,128)(2,1)} async-done(((bf16[768,3072]{1,0:T(8,128)(2,1)}), bf16[96,3072]{1,0:T(8,128)(2,1)}) %reduce-scatter.18.cloned.1.call-update) | async-done | bytes 589840 | tf_op jit(solution)/shard_map/reduce_scatter | solution.py:352
  675.4 38.4 %psum.127 = f32[]{:T(128)} all-reduce(f32[]{:T(128)} %get-tuple-element.442), channel_id=1, replica_groups=mesh['rep'=4,'cp'=8] {'rep','cp'}, use_global_device_ids=true, to_apply=%region_58.59 | all-reduce | flops 1 | bytes 8 | tf_op jit(solution)/shard_map/psum | solution.py:375
  713.9 26.8 %all-reduce.17 = (bf16[768]{0:T(1024)(128)(2,1)S(1)}, bf16[768]{0:T(1024)(128)(2,1)S(1)}, bf16[768]{0:T(1024)(128)(2,1)S(1)}, bf16[768]{0:T(1024)(128)(2,1)S(1)}...) all-reduce(bf16[768]{0:T(1024)(128)(2,1)S(1)} %copy-done.52, ...), channel_id=1, replica_groups=mesh['rep'=4,'cp'=8] {'cp'}, use_global_device_ids=true, to_apply=%add.7 | all-reduce | flops 9984 | bytes 39936
  741.4 10.0 %all-reduce.19 = (bf16[96]{0:T(256)(128)(2,1)S(1)}, bf16[96]{0:T(256)(128)(2,1)S(1)}, bf16[96]{0:T(256)(128)(2,1)S(1)}, bf16[96]{0:T(256)(128)(2,1)S(1)}, bf16[9...) all-reduce(bf16[96]{0:T(256)(128)(2,1)S(1)} %dynamic-slice.9, ...), channel_id=1, replica_groups=mesh['rep'=4,'cp'=8] {'rep'}, use_global_device_ids=true, to_apply=%region_22.23 | all-reduce | flops 1152 | bytes 4608 | tf_op jit(solution)/shard_map/psum | solution.py:373
  (321 shorter events, 131.3 us)
Async XLA Ops:
  7.2 52.3 %copy-start.7 = (bf16[1,256,768]{2,1,0:T(8,128)(2,1)S(1)}, bf16[1,256,768]{2,1,0:T(8,128)(2,1)}, u32[]{:S(2)}) copy-start(bf16[1,256,768]{2,1,0:T(8,128)(2,1)} %param.23) | copy-start | bytes 1179652
  7.2 41.0 %all-gather.9.cloned.1.call-start = ((), (), s32[]{:S(2)}) async-start(), calls=%async_computation.7 | async-start | bytes 1327104 | tf_op jit(solution)/shard_map/all_gather | solution.py:120
  7.9 51.5 %all-gather.13.cloned.1.call-start = ((), (), s32[]{:S(2)}) async-start(), calls=%async_computation.9 | async-start | bytes 1327104 | tf_op jit(solution)/shard_map/all_gather | solution.py:119
  8.7 130.4 %all-gather.15.cloned.1.call-start = ((), (), s32[]{:S(2)}) async-start(), calls=%async_computation.10 | async-start | bytes 1327104 | tf_op jit(solution)/shard_map/all_gather | solution.py:117
  9.4 208.2 %all-gather.11.cloned.1.call-start = ((), (), s32[]{:S(2)}) async-start(), calls=%async_computation.8 | async-start | bytes 3538944 | tf_op jit(solution)/shard_map/all_gather | solution.py:158
  48.2 67.8 %copy-start.57 = (bf16[384]{0:T(512)(128)(2,1)S(1)}, bf16[384]{0:T(512)(128)(2,1)}, u32[]{:S(2)}) copy-start(bf16[384]{0:T(512)(128)(2,1)} %param.34) | copy-start | bytes 2308
  50.8 196.3 %all-gather.17.cloned.1.call-start = ((), (), s32[]{:S(2)}) async-start(), calls=%async_computation.11 | async-start | bytes 1327104 | tf_op jit(solution)/shard_map/all_gather | solution.py:122
  51.4 198.8 %all-gather.19.cloned.1.call-start = ((), (), s32[]{:S(2)}) async-start(), calls=%async_computation.12 | async-start | bytes 5308416 | tf_op jit(solution)/shard_map/all_gather | solution.py:126
  52.0 214.5 %all-gather.21.cloned.1.call-start = ((), (), s32[]{:S(2)}) async-start(), calls=%async_computation.13 | async-start | bytes 5308416 | tf_op jit(solution)/shard_map/all_gather | solution.py:128
  62.0 8.4 %collective-permute-start = (bf16[256,768]{1,0:T(8,128)(2,1)S(1)}, bf16[256,768]{1,0:T(8,128)(2,1)S(1)}, u32[]{:S(2)}, u32[]{:S(2)}) collective-permute-start(bf16[256,768]{1,0:T(8,128)(2,1)S(1)} %get-tuple-element.434), channel_id=1, source_target_pairs={{0,7},{1,0},{2,1},{3,2},{4,3},{5,4},{6,5},{7,6},{8,15},{9,8},{10,9... | collective-permute-start | bytes 1179656 | tf_op jit(solution)/shard_map/ppermute | solution.py:90
  70.4 12.9 %collective-permute-start.1 = (bf16[256,768]{1,0:T(8,128)(2,1)S(1)}, bf16[256,768]{1,0:T(8,128)(2,1)S(1)}, u32[]{:S(2)}, u32[]{:S(2)}) collective-permute-start(bf16[256,768]{1,0:T(8,128)(2,1)S(1)} %collective-permute-done), channel_id=1, source_target_pairs={{0,7},{1,0},{2,1},{3,2},{4,3},{5,4},{6,5},{7,6},{8,15},{9,8},{10,9... | collective-permute-start | bytes 1179656 | tf_op jit(solution)/shard_map/ppermute | solution.py:90
  83.4 9.0 %collective-permute-start.2 = (bf16[256,768]{1,0:T(8,128)(2,1)S(1)}, bf16[256,768]{1,0:T(8,128)(2,1)S(1)}, u32[]{:S(2)}, u32[]{:S(2)}) collective-permute-start(bf16[256,768]{1,0:T(8,128)(2,1)S(1)} %collective-permute-done.1), channel_id=1, source_target_pairs={{0,7},{1,0},{2,1},{3,2},{4,3},{5,4},{6,5},{7,6},{8,15},{9,8},{10,9... | collective-permute-start | bytes 1179656 | tf_op jit(solution)/shard_map/ppermute | solution.py:90
  92.4 17.3 %collective-permute-start.3 = (bf16[256,768]{1,0:T(8,128)(2,1)S(1)}, bf16[256,768]{1,0:T(8,128)(2,1)S(1)}, u32[]{:S(2)}, u32[]{:S(2)}) collective-permute-start(bf16[256,768]{1,0:T(8,128)(2,1)S(1)} %collective-permute-done.2), channel_id=1, source_target_pairs={{0,7},{1,0},{2,1},{3,2},{4,3},{5,4},{6,5},{7,6},{8,15},{9,8},{10,9... | collective-permute-start | bytes 1179656 | tf_op jit(solution)/shard_map/ppermute | solution.py:90
  109.7 26.1 %collective-permute-start.4 = (bf16[256,768]{1,0:T(8,128)(2,1)S(1)}, bf16[256,768]{1,0:T(8,128)(2,1)S(1)}, u32[]{:S(2)}, u32[]{:S(2)}) collective-permute-start(bf16[256,768]{1,0:T(8,128)(2,1)S(1)} %collective-permute-done.3), channel_id=1, source_target_pairs={{0,7},{1,0},{2,1},{3,2},{4,3},{5,4},{6,5},{7,6},{8,15},{9,8},{10,9... | collective-permute-start | bytes 1179656 | tf_op jit(solution)/shard_map/ppermute | solution.py:90
  113.4 308.2 %reduce-scatter.14.cloned.1.call-start = ((), (), s32[]{:S(2)}) async-start(), calls=%async_computation.14 | async-start | bytes 7077888 | tf_op jit(solution)/shard_map/reduce_scatter | solution.py:284
  135.7 10.2 %collective-permute-start.5 = (bf16[256,768]{1,0:T(8,128)(2,1)S(1)}, bf16[256,768]{1,0:T(8,128)(2,1)S(1)}, u32[]{:S(2)}, u32[]{:S(2)}) collective-permute-start(bf16[256,768]{1,0:T(8,128)(2,1)S(1)} %collective-permute-done.4), channel_id=1, source_target_pairs={{0,7},{1,0},{2,1},{3,2},{4,3},{5,4},{6,5},{7,6},{8,15},{9,8},{10,9... | collective-permute-start | bytes 1179656 | tf_op jit(solution)/shard_map/ppermute | solution.py:90
  145.9 12.4 %collective-permute-start.6 = (bf16[256,768]{1,0:T(8,128)(2,1)S(1)}, bf16[256,768]{1,0:T(8,128)(2,1)S(1)}, u32[]{:S(2)}, u32[]{:S(2)}) collective-permute-start(bf16[256,768]{1,0:T(8,128)(2,1)S(1)} %collective-permute-done.5), channel_id=1, source_target_pairs={{0,7},{1,0},{2,1},{3,2},{4,3},{5,4},{6,5},{7,6},{8,15},{9,8},{10,9... | collective-permute-start | bytes 1179656 | tf_op jit(solution)/shard_map/ppermute | solution.py:90
  244.6 12.3 %copy-start.1 = (bf16[4,512,12,64]{1,3,2,0:T(8,128)(2,1)}, bf16[4,512,12,64]{1,3,2,0:T(8,128)(2,1)S(1)}, u32[]{:S(2)}) copy-start(bf16[4,512,12,64]{1,3,2,0:T(8,128)(2,1)S(1)} %get-tuple-element.697) | copy-start | bytes 9437188
  249.1 30.4 %copy-start.38 = (f32[256]{0:T(256)}, f32[256]{0:T(256)S(1)}, u32[]{:S(2)}) copy-start(f32[256]{0:T(256)S(1)} %broadcast_multiply_fusion.1) | copy-start | bytes 3076
  250.2 29.3 %copy-start.42 = (f32[256]{0:T(256)}, f32[256]{0:T(256)S(1)}, u32[]{:S(2)}) copy-start(f32[256]{0:T(256)S(1)} %fusion.52) | copy-start | bytes 3076
  250.2 16.3 %copy-start.29 = (f32[768]{0:T(1024)S(1)}, f32[768]{0:T(1024)}, u32[]{:S(2)}) copy-start(f32[768]{0:T(1024)} %convert_element_type.225) | copy-start | bytes 9220
  250.2 16.3 %copy-start.32 = (f32[768]{0:T(1024)S(1)}, f32[768]{0:T(1024)}, u32[]{:S(2)}) copy-start(f32[768]{0:T(1024)} %convert_element_type.226) | copy-start | bytes 9220
  250.2 16.3 %copy-start.54 = (f32[768]{0:T(1024)S(1)}, f32[768]{0:T(1024)}, u32[]{:S(2)}) copy-start(f32[768]{0:T(1024)} %convert_element_type.230) | copy-start | bytes 9220
  266.5 7.0 slice-start.2
  266.5 4.9 copy-start.9
  266.5 4.9 copy-start.34
  266.6 7.0 slice-start.3
  271.2 6.0 copy-start.36
  271.5 5.7 copy-start.40
  272.8 4.4 slice-start
  273.5 3.7 copy-start.21
  273.6 3.7 copy-start.3
  273.6 3.7 slice-start.1
  353.0 103.0 %reduce-scatter.22.cloned.1.call-start = ((), (), s32[]{:S(2)}) async-start(), calls=%async_computation.18 | async-start | bytes 1327104
  357.0 132.8 %reduce-scatter.24.cloned.1.call-start = ((), (), s32[]{:S(2)}) async-start(), calls=%async_computation.19 | async-start | bytes 1327104
  421.6 3.1 copy-start.13
  424.7 98.7 %reduce-scatter.26.cloned.1.call-start = ((), (), s32[]{:S(2)}) async-start(), calls=%async_computation.20 | async-start | bytes 1327104
  425.3 3.4 copy-start.22
  426.8 130.1 %reduce-scatter.16.cloned.1.call-start = ((), (), s32[]{:S(2)}) async-start(), calls=%async_computation.15 | async-start | bytes 1327104 | tf_op jit(solution)/shard_map/reduce_scatter | solution.py:340
  428.4 183.9 %reduce-scatter.20.cloned.1.call-start = ((), (), s32[]{:S(2)}) async-start(), calls=%async_computation.17 | async-start | bytes 5308416 | tf_op jit(solution)/shard_map/reduce_scatter | solution.py:358
  433.8 234.0 %reduce-scatter.18.cloned.1.call-start = ((), (), s32[]{:S(2)}) async-start(), calls=%async_computation.16 | async-start | bytes 5308416 | tf_op jit(solution)/shard_map/reduce_scatter | solution.py:352
  440.1 227.7 %copy-start.10 = (f32[1,256,768]{2,1,0:T(8,128)S(1)}, f32[1,256,768]{2,1,0:T(8,128)}, u32[]{:S(2)}) copy-start(f32[1,256,768]{2,1,0:T(8,128)} %param.39) | copy-start | bytes 2359300
  440.1 229.7 %copy-start.58 = (bf16[96]{0:T(256)(128)(2,1)S(1)}, bf16[96]{0:T(256)(128)(2,1)}, u32[]{:S(2)}) copy-start(bf16[96]{0:T(256)(128)(2,1)} %param.38) | copy-start | bytes 580
  440.1 230.6 %copy-start.12 = (f32[256,768]{1,0:T(8,128)S(1)}, f32[256,768]{1,0:T(8,128)}, u32[]{:S(2)}) copy-start(f32[256,768]{1,0:T(8,128)} %copy-done.11) | copy-start | bytes 2359300
  440.1 230.6 %copy-start.45 = (f32[256]{0:T(256)S(1)}, f32[256]{0:T(256)}, u32[]{:S(2)}) copy-start(f32[256]{0:T(256)} %copy-done.44) | copy-start | bytes 3076
  440.1 317.8 %all-reduce.23.cloned.1.call-start = ((), (), s32[]{:S(2)}) async-start(), calls=%async_computation.21 | async-start | bytes 3833856 | tf_op jit(solution)/shard_map/psum | solution.py:373
  491.5 181.2 %copy-start.14 = (bf16[768,768]{1,0:T(8,128)(2,1)S(1)}, bf16[768,768]{1,0:T(8,128)(2,1)}, u32[]{:S(2)}) copy-start(bf16[768,768]{1,0:T(8,128)(2,1)} %all-gather.13.cloned.1.call-done) | copy-start | bytes 3538948
  672.7 41.1 %copy-start.46 = (bf16[768]{0:T(1024)(128)(2,1)S(1)}, bf16[768]{0:T(1024)(128)(2,1)}, u32[]{:S(2)}) copy-start(bf16[768]{0:T(1024)(128)(2,1)} %get-tuple-element.336) | copy-start | bytes 4612
  672.8 84.0 %copy-start.6 = (f32[256,768]{1,0:T(8,128)S(1)}, f32[256,768]{1,0:T(8,128)}, u32[]{:S(2)}) copy-start(f32[256,768]{1,0:T(8,128)} %copy-done.5) | copy-start | bytes 2359300
  672.8 84.0 %copy-start.35 = (f32[768]{0:T(1024)S(1)}, f32[768]{0:T(1024)}, u32[]{:S(2)}) copy-start(f32[768]{0:T(1024)} %convert_element_type.231) | copy-start | bytes 9220
  672.8 84.0 %copy-start.37 = (f32[256]{0:T(256)S(1)}, f32[256]{0:T(256)}, u32[]{:S(2)}) copy-start(f32[256]{0:T(256)} %copy-done.36) | copy-start | bytes 3076
  672.8 84.0 %copy-start.41 = (f32[256]{0:T(256)S(1)}, f32[256]{0:T(256)}, u32[]{:S(2)}) copy-start(f32[256]{0:T(256)} %copy-done.40) | copy-start | bytes 3076
  673.3 40.6 %copy-start.47 = (bf16[768]{0:T(1024)(128)(2,1)S(1)}, bf16[768]{0:T(1024)(128)(2,1)}, u32[]{:S(2)}) copy-start(bf16[768]{0:T(1024)(128)(2,1)} %get-tuple-element.417) | copy-start | bytes 4612
  673.3 40.6 %copy-start.48 = (bf16[768]{0:T(1024)(128)(2,1)S(1)}, bf16[768]{0:T(1024)(128)(2,1)}, u32[]{:S(2)}) copy-start(bf16[768]{0:T(1024)(128)(2,1)} %get-tuple-element.421) | copy-start | bytes 4612
  673.3 40.6 %copy-start.49 = (bf16[768]{0:T(1024)(128)(2,1)S(1)}, bf16[768]{0:T(1024)(128)(2,1)}, u32[]{:S(2)}) copy-start(bf16[768]{0:T(1024)(128)(2,1)} %reduce_sum.263) | copy-start | bytes 4612
  673.4 40.5 %copy-start.50 = (bf16[768]{0:T(1024)(128)(2,1)S(1)}, bf16[768]{0:T(1024)(128)(2,1)}, u32[]{:S(2)}) copy-start(bf16[768]{0:T(1024)(128)(2,1)} %reduce_sum.224) | copy-start | bytes 4612
  673.4 40.5 %copy-start.52 = (bf16[768]{0:T(1024)(128)(2,1)S(1)}, bf16[768]{0:T(1024)(128)(2,1)}, u32[]{:S(2)}) copy-start(bf16[768]{0:T(1024)(128)(2,1)} %copy-done.51) | copy-start | bytes 4612
  673.4 40.5 %copy-start.53 = (bf16[3072]{0:T(1024)(128)(2,1)S(1)}, bf16[3072]{0:T(1024)(128)(2,1)}, u32[]{:S(2)}) copy-start(bf16[3072]{0:T(1024)(128)(2,1)} %get-tuple-element.419) | copy-start | bytes 18436
  673.4 40.5 %copy-start.55 = (bf16[768]{0:T(1024)(128)(2,1)S(1)}, bf16[768]{0:T(1024)(128)(2,1)}, u32[]{:S(2)}) copy-start(bf16[768]{0:T(1024)(128)(2,1)} %get-tuple-element.338) | copy-start | bytes 4612
  673.4 40.5 %copy-start.56 = (bf16[768]{0:T(1024)(128)(2,1)S(1)}, bf16[768]{0:T(1024)(128)(2,1)}, u32[]{:S(2)}) copy-start(bf16[768]{0:T(1024)(128)(2,1)} %get-tuple-element.340) | copy-start | bytes 4612
  757.9 4.4 copy-start.31
  757.9 5.2 copy-start.28
  757.9 6.0 copy-start.27
  757.9 6.9 copy-start.26
  (25 other events, 42.9 us)
Sparse Core Ops, SparseCore 0:
  9.6 25.6 all-gather.8
  37.0 22.4 all-gather.12
  61.1 25.6 all-gather.14
  88.9 42.3 all-gather.10
  132.8 28.6 all-gather.16
  163.0 51.8 all-gather.18
  216.5 49.9 all-gather.20
  353.1 68.4 reduce-scatter.13
  424.5 31.4 reduce-scatter.21
  458.7 31.0 reduce-scatter.23
  492.1 31.2 reduce-scatter.25
  525.5 31.3 reduce-scatter.15
  559.2 53.0 reduce-scatter.19
  614.5 53.3 reduce-scatter.17
  672.1 66.5 all-reduce.22
